TPU v7x, 32 devices: a whole 2x2x4 slice. The times are simulated.
32 devices in a mesh: parts: 2 (over y), tm: 4 (over z), sub: 2 (over x), inner: 2 (over core).
Axes of the slice: x: 2, y: 2, z: 4, core: 2. Of those that a mesh axis runs over, the one named last changes fastest.
Arguments:
- guess: float32 [512, 128], P(('parts', 'tm', 'sub', 'inner')), parts along dimension 0, may hold values from -6 to 6
- start: float32 [256], P('parts'), parts along dimension 0, may hold values from -6 to 6
- layer_weight: float32 [256, 64], replicated, may hold values from -0.75 to 0.75
- layer_bias: float32 [256], replicated, may hold values from -4 to 4
- amplitude: float32 [256], replicated, may hold values from 0.5 to 4
Outputs:
- updated: float32 [512, 128], P(('parts', 'tm', 'sub', 'inner')), parts along dimension 0
There are 2 independent parts, one for each index of `parts`. A program takes and returns all parts, laid end to end along the dimension named above; an argument that names none is the same for every part. Nothing has to cross between parts.
All inputs are finite; a program needn't handle non-finite values.
Results may differ from a plain program's by a relative error of at most 0.0003.
Values sent between devices are 32-bit elements; how exact they have to be, the bound alone decides.
No kernel may reach another device: no remote copies, remote signals or barrier semaphores. Data moves between devices by JAX's collectives and lax.ppermute only.
A program may use at most 128 MiB of HBM per device.

v0:
```python
import jax
import jax.numpy as jnp
from jax import lax
from jax.sharding import PartitionSpec as P

step_size = 0.04
curvature = 0.5


def from_behind(value, axis, steps):
    count = lax.axis_size(axis)
    first, last = (max(0, -steps), min(count, count - steps))
    return lax.ppermute(value, axis, [(source, source + steps) for source in range(first, last)])


def carried_in(value, axis, join, neutral):
    count, mine = (lax.axis_size(axis), lax.axis_index(axis))
    pieces = jax.tree.map(lambda part: lax.all_gather(part, axis), value)
    running = jax.tree.map(
        lambda part, zero: jnp.full_like(part, 0) + jnp.asarray(zero, part.dtype), value, neutral
    )

    def turn(position, running):
        longer = join(running, jax.tree.map(lambda part: part[position], pieces))
        return jax.tree.map(lambda new, old: jnp.where(position < mine, new, old), longer, running)

    return lax.fori_loop(0, count - 1, turn, running)


def broadcast(shard, axis, root):
    mine = lax.axis_index(axis) == root
    return lax.psum(jnp.where(mine, shard, jnp.zeros_like(shard)), axis)


def forces(coords, layer_weight, layer_bias, amplitude):
    hi = lax.Precision.HIGHEST
    pre = jnp.dot(coords, layer_weight.T, precision=hi) + layer_bias
    gate = jax.nn.sigmoid(pre)
    grad = jnp.dot(amplitude * gate, layer_weight, precision=hi) + curvature * coords
    return (grad, amplitude * gate * (1.0 - gate))


def hess_apply(vector, layer_weight, weights_d):
    hi = lax.Precision.HIGHEST
    inner_vals = jnp.dot(layer_weight, vector, precision=hi) * weights_d
    return jnp.dot(inner_vals, layer_weight, precision=hi) + curvature * vector


def hessian(layer_weight, weights_d):
    hi = lax.Precision.HIGHEST
    width = layer_weight.shape[1]
    scaled = layer_weight * weights_d[:, None]
    return jnp.dot(scaled.T, layer_weight, precision=hi) + curvature * jnp.eye(
        width, dtype=jnp.float32
    )


def combine(earlier, later):
    hi = lax.Precision.HIGHEST
    map_early, shift_early = earlier
    map_late, shift_late = later
    return (
        jnp.dot(map_late, map_early, precision=hi),
        jnp.dot(map_late, shift_early, precision=hi) + shift_late,
    )


def shards(guess, start, layer_weight, layer_bias, amplitude):
    hi = lax.Precision.HIGHEST
    width = layer_weight.shape[1]
    state_len = 2 * width
    received = from_behind(guess[-1], ("tm", "sub", "inner"), 1)
    previous = jnp.where(lax.axis_index(("tm", "sub", "inner")) == 0, start, received)
    before = jnp.concatenate([previous[None, :], guess[:-1]], axis=0)
    coords, momenta = (before[:, :width], before[:, width:])
    grad_zero, curve_zero = forces(coords, layer_weight, layer_bias, amplitude)
    half = momenta - 0.5 * step_size * grad_zero
    moved = coords + step_size * half
    grad_one, curve_one = forces(moved, layer_weight, layer_bias, amplitude)
    landed = half - 0.5 * step_size * grad_one
    image = jnp.concatenate([moved, landed], axis=1)
    unit = jnp.eye(width, dtype=jnp.float32)

    def compose(carry, items):
        window_map, window_shift = carry
        prior, curve_a, curve_b, target = items
        hess_a = hessian(layer_weight, curve_a)
        hess_b = hessian(layer_weight, curve_b)
        block_qq = unit - 0.5 * step_size * step_size * hess_a
        block_pq = -0.5 * step_size * (hess_a + jnp.dot(hess_b, block_qq, precision=hi))
        block_pp = unit - 0.5 * step_size * step_size * hess_b
        jacobian = jnp.block([[block_qq, step_size * unit], [block_pq, block_pp]])
        offset = target - jnp.dot(jacobian, prior, precision=hi)
        new_map = jnp.dot(jacobian, window_map, precision=hi)
        new_shift = jnp.dot(jacobian, window_shift, precision=hi) + offset
        return ((new_map, new_shift), None)

    identity = (jnp.eye(state_len, dtype=jnp.float32), jnp.zeros((state_len,), jnp.float32))
    local, unused = lax.scan(compose, identity, (before, curve_zero, curve_one, image))
    lower = carried_in(local, ("sub", "inner"), combine, identity)
    closing = combine(lower, local)
    total = (
        broadcast(closing[0], ("sub", "inner"), lax.axis_size(("sub", "inner")) - 1),
        broadcast(closing[1], ("sub", "inner"), lax.axis_size(("sub", "inner")) - 1),
    )
    major = carried_in(total, "tm", combine, identity)
    prefix = combine(major, lower)
    entering = jnp.dot(prefix[0], start, precision=hi) + prefix[1]

    def advance(state, items):
        prior, curve_a, curve_b, target = items
        delta = state - prior
        delta_q, delta_p = (delta[:width], delta[width:])
        first = hess_apply(delta_q, layer_weight, curve_a)
        new_q = delta_q - 0.5 * step_size * step_size * first + step_size * delta_p
        new_p = (
            delta_p
            - 0.5 * step_size * first
            - 0.5 * step_size * hess_apply(new_q, layer_weight, curve_b)
        )
        result = target + jnp.concatenate([new_q, new_p])
        return (result, result)

    final, states = lax.scan(advance, entering, (before, curve_zero, curve_one, image))
    return states


def solution(mesh):
    placed = (P(("parts", "tm", "sub", "inner"), None), P("parts"), P(), P(), P())
    return jax.shard_map(
        shards,
        mesh=mesh,
        in_specs=placed,
        out_specs=P(("parts", "tm", "sub", "inner"), None),
        check_vma=False,
    )
```

profile of v0, /device:TPU:0, one launch (start us, length us, event | category | flops | bytes accessed | tf_op | source)
XLA Modules:
  0.0 143.9 jit_solution(9281563523348621520)
XLA Ops:
  6.5 0.7 slice_bitcast_fusion
  7.2 2.4 %collective-permute-start = (f32[128]{0:T(128)S(1)}, f32[128]{0:T(128)S(1)}, u32[]{:S(2)}, u32[]{:S(2)}) collective-permute-start(f32[128]{0:T(128)S(1)} %slice_bitcast_fusion), channel_id=1, source_target_pairs={{0,1},{1,2},{2,3},{3,4},{4,5},{5,6},{6,7},{7,8},{8,9},{9,10},{10,1... | collective-permute-start | bytes 1544 | tf_op jit(solution)/shard_map/ppermute | solution.py:13
  9.7 0.6 copy-done.1
  11.1 0.5 copy-done.9
  12.9 0.6 copy-done.5
  13.5 24.4 %while.61 = (s32[]{:T(128)}, f32[128,128]{1,0:T(8,128)S(1)}, f32[128]{0:T(128)S(1)}, f32[16,256]{1,0:T(8,128)S(1)}, f32[256,64]{0,1:T(8,128)S(1)}, /*index=5*/f3...) while((s32[]{:T(128)}, f32[128,128]{1,0:T(8,128)S(1)}, ...), condition=%wide.region_1.2_spmd.clone.clone, body=%wide.region_0.1_spmd.clone.clone.sunk | while | flops 54133120 | bytes 797811 | solution.py:99
  37.9 8.5 %all-gather = f32[512,128]{1,0:T(8,128)S(1)} all-gather(f32[128,128]{1,0:T(8,128)S(1)} %get-tuple-element.321), channel_id=2, replica_groups=mesh['parts'=2,'tm'=4,'sub'=2,'inner'=2] {'sub','inner'}, dimensions={0}, use_global_device_ids=true | all-gather | bytes 327680 | tf_op jit(solution)/shard_map/all_gather | solution.py:18
  46.4 5.0 %all-gather.2 = f32[4,1,128]{2,1,0:T(1,128)S(1)} all-gather(f32[1,1,128]{2,1,0:T(1,128)S(1)} %bitcast.249), channel_id=3, replica_groups=mesh['parts'=2,'tm'=4,'sub'=2,'inner'=2] {'sub','inner'}, dimensions={0}, use_global_device_ids=true | all-gather | bytes 2560 | tf_op jit(solution)/shard_map/all_gather | solution.py:18
  51.4 1.4 while.59
  52.9 0.8 fusion.52
  53.9 7.1 %psum.15 = f32[1,128]{1,0:T(1,128)S(1)} all-reduce(f32[1,128]{1,0:T(1,128)S(1)} %fusion.68), channel_id=1, replica_groups=mesh['parts'=2,'tm'=4,'sub'=2,'inner'=2] {'sub','inner'}, use_global_device_ids=true, to_apply=%region_5.6 | all-reduce | flops 128 | bytes 1024 | tf_op jit(solution)/shard_map/psum | solution.py:32
  61.1 11.1 %all-gather.3 = f32[4,1,128]{2,1,0:T(1,128)S(1)} all-gather(f32[1,1,128]{2,1,0:T(1,128)S(1)} %bitcast.250), channel_id=1, replica_groups=mesh['parts'=2,'tm'=4,'sub'=2,'inner'=2] {'tm'}, dimensions={0}, use_global_device_ids=true | all-gather | bytes 2560 | tf_op jit(solution)/shard_map/all_gather | solution.py:18
  72.2 14.5 %all-reduce.2.cloned.1.call-done = f32[1,128,128]{2,1,0:T(8,128)} async-done(((f32[1,128,128]{2,1,0:T(8,128)}), f32[1,128,128]{2,1,0:T(8,128)}) %all-reduce.2.cloned.1.call-update) | async-done | bytes 65552 | tf_op jit(solution)/shard_map/psum | solution.py:32
  86.7 14.1 %all_gather.29 = f32[4,128,128]{2,1,0:T(8,128)S(1)} all-gather(f32[1,128,128]{2,1,0:T(8,128)} %all-reduce.2.cloned.1.call-done), channel_id=1, replica_groups=mesh['parts'=2,'tm'=4,'sub'=2,'inner'=2] {'tm'}, dimensions={0}, use_global_device_ids=true | all-gather | bytes 327680 | tf_op jit(solution)/shard_map/all_gather | solution.py:18
  100.8 1.4 while.60
  102.8 34.2 %while.58 = (s32[]{:T(128)}, f32[128]{0:T(128)S(1)}, f32[16,128]{1,0:T(8,128)}, f32[16,128]{1,0:T(8,128)S(1)}, f32[16,128]{1,0:T(8,128)S(1)}, /*index=5*/f32[256...) while((s32[]{:T(128)}, f32[128]{0:T(128)S(1)}, ...), condition=%wide.region_9.10_spmd, body=%wide.region_8.9_spmd.sunk | while | flops 788354 | bytes 285049 | solution.py:124
  103.6 1.3 dynamic_update_slice.5
  105.8 1.3 dynamic_update_slice.5
  107.9 1.3 dynamic_update_slice.5
  110.0 1.3 dynamic_update_slice.5
  112.2 1.3 dynamic_update_slice.5
  114.3 1.3 dynamic_update_slice.5
  116.5 1.3 dynamic_update_slice.5
  118.6 1.3 dynamic_update_slice.5
  120.7 1.3 dynamic_update_slice.5
  122.9 1.3 dynamic_update_slice.5
  125.0 1.3 dynamic_update_slice.5
  127.1 1.3 dynamic_update_slice.5
  129.3 1.3 dynamic_update_slice.5
  131.4 1.3 dynamic_update_slice.5
  133.6 1.3 dynamic_update_slice.5
  135.7 1.3 dynamic_update_slice.5
  (381 shorter events, 42.0 us)
Async XLA Ops:
  6.5 80.2 %all-reduce.2.cloned.1.call-start = ((), (), s32[]{:S(2)}) async-start(), calls=%async_computation | async-start | bytes 131072 | tf_op jit(solution)/shard_map/psum | solution.py:32
  7.2 3.2 %collective-permute-start = (f32[128]{0:T(128)S(1)}, f32[128]{0:T(128)S(1)}, u32[]{:S(2)}, u32[]{:S(2)}) collective-permute-start(f32[128]{0:T(128)S(1)} %slice_bitcast_fusion), channel_id=1, source_target_pairs={{0,1},{1,2},{2,3},{3,4},{4,5},{5,6},{6,7},{7,8},{8,9},{9,10},{10,1... | collective-permute-start | bytes 1544 | tf_op jit(solution)/shard_map/ppermute | solution.py:13
  9.6 0.6 copy-start.1
  10.3 0.8 copy-start
  10.3 0.8 copy-start.7
  10.3 0.7 copy-start.10
  11.0 0.7 copy-start.9
  11.7 0.7 copy-start.8
  12.7 0.8 copy-start.5
  37.9 13.6 %copy-start.6 = (f32[128,128]{1,0:T(8,128)S(1)}, f32[128,128]{1,0:T(8,128)}, u32[]{:S(2)}) copy-start(f32[128,128]{1,0:T(8,128)} %copy-done.1) | copy-start | bytes 196612
  52.9 0.8 copy-start.3
  72.2 28.5 %copy-start.2 = (f32[128,128]{1,0:T(8,128)S(1)}, f32[128,128]{1,0:T(8,128)}, u32[]{:S(2)}) copy-start(f32[128,128]{1,0:T(8,128)} %copy-done.1) | copy-start | bytes 196612
  100.8 1.4 %copy-start.4 = (f32[128,128]{1,0:T(8,128)S(1)}, f32[128,128]{1,0:T(8,128)}, u32[]{:S(2)}) copy-start(f32[128,128]{1,0:T(8,128)} %copy-done.3) | copy-start | bytes 196612
Sparse Core Ops, SparseCore 0:
  53.9 32.7 all-reduce.1
where the time goes:
time: 145 us; the launch traced here: 144 us
  blocking collectives  45.9 us (32%)
  matrix products  36.6 us (25%)
  local copies, waits for them, and re-layouts  25.9 us (18%)
  waiting for transfers between devices  14.6 us (10%)
  between operations  13.5 us (9%)
  other arithmetic  3.46 us (2%)
  starting transfers between devices  2.39 us (2%)
  loops' own time  1.58 us (1%)
    all_gather x4, blocking collectives, carried_in(): pieces = jax.tree.map(lambda part: lax.all_gather(part, axis), value)  38.7 us
    dynamic_update_slice x16, local copies, waits for them, and re-layouts, shards(): lax.scan(advance, entering, (before, curve_zero, curve_one, image))  20.8 us
    psum x1, waiting for transfers between devices, broadcast(): return lax.psum(jnp.where(mine, shard, jnp.zeros_like(shard)), axis)  14.5 us
    psum x1, blocking collectives, broadcast(): return lax.psum(jnp.where(mine, shard, jnp.zeros_like(shard)), axis)  7.14 us
    dot_general x32, matrix products, hessian(): jnp.dot(scaled.T, layer_weight, precision=hi)  6.57 us
    dot_general x32, matrix products, hess_apply(): inner_vals = jnp.dot(layer_weight, vector, precision=hi) * weights_d  4.9 us
    dot_general x32, matrix products, hess_apply(): return jnp.dot(inner_vals, layer_weight, precision=hi) + curvature * vector  4.78 us
    dot_general x16, matrix products, compose(): new_shift = jnp.dot(jacobian, window_shift, precision=hi) + offset  4.76 us
  transfers between devices with their start and end apart: 2, of which 2 were waited for; matrix products, arithmetic and copies ran while one was open for 0% of the time, Pallas kernels for 0%

commit v1 on v0

--- a/solution.py
+++ b/solution.py
@@ -29,7 +29,7 @@
 
 def broadcast(shard, axis, root):
     mine = lax.axis_index(axis) == root
-    return lax.psum(jnp.where(mine, shard, jnp.zeros_like(shard)), axis)
+    return jnp.sum(lax.all_gather(jnp.where(mine, shard, jnp.zeros_like(shard)), axis), axis=0)
 
 
 def forces(coords, layer_weight, layer_bias, amplitude):

time: 145 us -> 122 us (0.84)
  waiting for transfers between devices: 14.6 us -> 0.13 us
  between operations: 13.5 us -> 0.18 us
  blocking collectives: 45.9 us -> 51 us
    psum x1 -> x0, waiting for transfers between devices: 14.5 us -> none  [broadcast(): return lax.psum(jnp.where(mine, shard, jnp.zeros_like(shard)), axis)]
    all_gather x0 -> x2, blocking collectives: none -> 10.9 us  [broadcast(): lax.all_gather(jnp.where(mine, shard, jnp.zeros_like(shard)), axis)]
    psum x1 -> x0, blocking collectives: 7.14 us -> none  [broadcast(): return lax.psum(jnp.where(mine, shard, jnp.zeros_like(shard)), axis)]
  transfers between devices with their start and end apart: 2 -> 1, of which waited for: 2 -> 1; matrix products, arithmetic and copies ran while one was open for 0% -> 0% of each run, Pallas kernels for 0% -> 0%
where the time goes in v1:
time: 122 us; the launch traced here: 121 us
  blocking collectives  51 us (42%)
  matrix products  35.9 us (29%)
  local copies, waits for them, and re-layouts  25.9 us (21%)
  other arithmetic  3.5 us (3%)
  starting transfers between devices  2.38 us (2%)
  loops' own time  1.58 us (1%)
    all_gather x4, blocking collectives, carried_in(): pieces = jax.tree.map(lambda part: lax.all_gather(part, axis), value)  40.1 us
    dynamic_update_slice x16, local copies, waits for them, and re-layouts, shards(): lax.scan(advance, entering, (before, curve_zero, curve_one, image))  20.8 us
    all_gather x2, blocking collectives, broadcast(): lax.all_gather(jnp.where(mine, shard, jnp.zeros_like(shard)), axis)  10.9 us
    dot_general x32, matrix products, hessian(): jnp.dot(scaled.T, layer_weight, precision=hi)  6.57 us
    dot_general x32, matrix products, hess_apply(): inner_vals = jnp.dot(layer_weight, vector, precision=hi) * weights_d  4.9 us
    dot_general x32, matrix products, hess_apply(): return jnp.dot(inner_vals, layer_weight, precision=hi) + curvature * vector  4.78 us
    dot_general x16, matrix products, compose(): new_shift = jnp.dot(jacobian, window_shift, precision=hi) + offset  4.76 us
    dot_general x16, matrix products, compose(): new_map = jnp.dot(jacobian, window_map, precision=hi)  4.19 us
  transfers between devices with their start and end apart: 1, of which 1 were waited for; matrix products, arithmetic and copies ran while one was open for 0% of the time, Pallas kernels for 0%

profile of v1, /device:TPU:0, one launch (start us, length us, event | category | flops | bytes accessed | tf_op | source)
XLA Modules:
  0.0 120.6 jit_solution(9716836365526809322)
XLA Ops:
  0.0 0.7 slice_bitcast_fusion
  0.7 2.4 %collective-permute-start = (f32[128]{0:T(128)S(1)}, f32[128]{0:T(128)S(1)}, u32[]{:S(2)}, u32[]{:S(2)}) collective-permute-start(f32[128]{0:T(128)S(1)} %slice_bitcast_fusion), channel_id=1, source_target_pairs={{0,1},{1,2},{2,3},{3,4},{4,5},{5,6},{6,7},{7,8},{8,9},{9,10},{10,1... | collective-permute-start | bytes 1544 | tf_op jit(solution)/shard_map/ppermute | solution.py:13
  3.1 0.6 copy-done.1
  3.9 0.5 copy-done.10
  4.6 0.5 copy-done.9
  6.4 0.6 copy-done.5
  7.0 24.4 %while.61 = (s32[]{:T(128)}, f32[128,128]{1,0:T(8,128)S(1)}, f32[128]{0:T(128)S(1)}, f32[16,256]{1,0:T(8,128)S(1)}, f32[256,64]{0,1:T(8,128)S(1)}, /*index=5*/f3...) while((s32[]{:T(128)}, f32[128,128]{1,0:T(8,128)S(1)}, ...), condition=%wide.region_1.2_spmd.clone.clone, body=%wide.region_0.1_spmd.clone.clone.sunk | while | flops 54133120 | bytes 797811 | solution.py:99
  31.4 8.5 %all-gather = f32[512,128]{1,0:T(8,128)S(1)} all-gather(f32[128,128]{1,0:T(8,128)S(1)} %get-tuple-element.321), channel_id=2, replica_groups=mesh['parts'=2,'tm'=4,'sub'=2,'inner'=2] {'sub','inner'}, dimensions={0}, use_global_device_ids=true | all-gather | bytes 327680 | tf_op jit(solution)/shard_map/all_gather | solution.py:18
  39.9 5.0 %all-gather.6 = f32[4,1,128]{2,1,0:T(1,128)S(1)} all-gather(f32[1,1,128]{2,1,0:T(1,128)S(1)} %bitcast.251), channel_id=3, replica_groups=mesh['parts'=2,'tm'=4,'sub'=2,'inner'=2] {'sub','inner'}, dimensions={0}, use_global_device_ids=true | all-gather | bytes 2560 | tf_op jit(solution)/shard_map/all_gather | solution.py:18
  44.9 1.4 %while.59 = (s32[]{:T(128)}, f32[128,128]{1,0:T(8,128)S(1)}, f32[128]{0:T(128)S(1)}, s32[]{:T(128)}, f32[4,128,128]{2,1,0:T(8,128)S(1)}, /*index=5*/f32[4,128]{1,0:T(4,128)S(1)}, s32[]{:T(128)}, s32[]{:T(128)}) while((s32[]{:T(128)}, f32[128,128]{1,0:T(8,128)S(1)}, f32[128]{0:T(128)S(1)}, s32[]{:T(128)}, ...), condition=%wide.region_3.4_spmd.clone, body=%wide.region_2.3_spmd.clone.sunk | while | flops 25379332 | bytes 464492 | solution.py:27
  46.5 5.1 %all-gather.7 = f32[4,1,128]{2,1,0:T(1,128)S(1)} all-gather(f32[1,1,128]{2,1,0:T(1,128)S(1)} %fusion.67), channel_id=6, replica_groups=mesh['parts'=2,'tm'=4,'sub'=2,'inner'=2] {'sub','inner'}, dimensions={0}, use_global_device_ids=true | all-gather | bytes 2560 | tf_op jit(solution)/shard_map/all_gather | solution.py:32
  51.6 12.1 %all-gather.8 = f32[4,1,128]{2,1,0:T(1,128)S(1)} all-gather(f32[1,1,128]{2,1,0:T(1,128)S(1)} %bitcast.252), channel_id=7, replica_groups=mesh['parts'=2,'tm'=4,'sub'=2,'inner'=2] {'tm'}, dimensions={0}, use_global_device_ids=true | all-gather | bytes 2560 | tf_op jit(solution)/shard_map/all_gather | solution.py:18
  64.0 5.8 %all-gather.2 = f32[512,128]{1,0:T(8,128)S(1)} all-gather(f32[128,128]{1,0:T(8,128)S(1)} %convolution_select_fusion.2), channel_id=4, replica_groups=mesh['parts'=2,'tm'=4,'sub'=2,'inner'=2] {'sub','inner'}, dimensions={0}, use_global_device_ids=true | all-gather | bytes 327680 | tf_op jit(solution)/shard_map/all_gather | solution.py:32
  69.8 14.5 %all-gather.3 = f32[512,128]{1,0:T(8,128)S(1)} all-gather(f32[128,128]{1,0:T(8,128)S(1)} %reduce_sum.18), channel_id=5, replica_groups=mesh['parts'=2,'tm'=4,'sub'=2,'inner'=2] {'tm'}, dimensions={0}, use_global_device_ids=true | all-gather | bytes 327680 | tf_op jit(solution)/shard_map/all_gather | solution.py:18
  84.3 1.4 %while.60 = (s32[]{:T(128)}, f32[128,128]{1,0:T(8,128)S(1)}, f32[128]{0:T(128)S(1)}, s32[]{:T(128)}, f32[4,128,128]{2,1,0:T(8,128)S(1)}, /*index=5*/f32[4,128]{1,0:T(4,128)S(1)}, s32[]{:T(128)}, s32[]{:T(128)}) while((s32[]{:T(128)}, f32[128,128]{1,0:T(8,128)S(1)}, f32[128]{0:T(128)S(1)}, s32[]{:T(128)}, ...), condition=%wide.region_7.8_spmd.clone, body=%wide.region_6.7_spmd.clone.sunk | while | flops 25379332 | bytes 464492 | solution.py:27
  86.3 34.2 %while.58 = (s32[]{:T(128)}, f32[128]{0:T(128)S(1)}, f32[16,128]{1,0:T(8,128)}, f32[16,128]{1,0:T(8,128)S(1)}, f32[16,128]{1,0:T(8,128)S(1)}, /*index=5*/f32[256...) while((s32[]{:T(128)}, f32[128]{0:T(128)S(1)}, ...), condition=%wide.region_9.10_spmd, body=%wide.region_8.9_spmd.sunk | while | flops 788354 | bytes 285049 | solution.py:124
  87.2 1.3 %dynamic_update_slice.5 = f32[16,128]{1,0:T(8,128)} dynamic-update-slice(f32[16,128]{1,0:T(8,128)} %get-tuple-element.777, f32[1,128]{1,0:T(1,128)S(1)} %maximum_add_fusion.5, s32[]{:T(128)} %get-tuple-element.775, s32[]{:T(128)} %constant.104.clone.1..sunk) | dynamic-update-slice | bytes 1028 | tf_op jit(solution)/shard_map/while/body/jit(dynamic_update_index_in_dim)/dynamic_update_slice | solution.py:124
  89.3 1.3 %dynamic_update_slice.5 = f32[16,128]{1,0:T(8,128)} dynamic-update-slice(f32[16,128]{1,0:T(8,128)} %get-tuple-element.777, f32[1,128]{1,0:T(1,128)S(1)} %maximum_add_fusion.5, s32[]{:T(128)} %get-tuple-element.775, s32[]{:T(128)} %constant.104.clone.1..sunk) | dynamic-update-slice | bytes 1028 | tf_op jit(solution)/shard_map/while/body/jit(dynamic_update_index_in_dim)/dynamic_update_slice | solution.py:124
  91.4 1.3 %dynamic_update_slice.5 = f32[16,128]{1,0:T(8,128)} dynamic-update-slice(f32[16,128]{1,0:T(8,128)} %get-tuple-element.777, f32[1,128]{1,0:T(1,128)S(1)} %maximum_add_fusion.5, s32[]{:T(128)} %get-tuple-element.775, s32[]{:T(128)} %constant.104.clone.1..sunk) | dynamic-update-slice | bytes 1028 | tf_op jit(solution)/shard_map/while/body/jit(dynamic_update_index_in_dim)/dynamic_update_slice | solution.py:124
  93.6 1.3 %dynamic_update_slice.5 = f32[16,128]{1,0:T(8,128)} dynamic-update-slice(f32[16,128]{1,0:T(8,128)} %get-tuple-element.777, f32[1,128]{1,0:T(1,128)S(1)} %maximum_add_fusion.5, s32[]{:T(128)} %get-tuple-element.775, s32[]{:T(128)} %constant.104.clone.1..sunk) | dynamic-update-slice | bytes 1028 | tf_op jit(solution)/shard_map/while/body/jit(dynamic_update_index_in_dim)/dynamic_update_slice | solution.py:124
  95.7 1.3 %dynamic_update_slice.5 = f32[16,128]{1,0:T(8,128)} dynamic-update-slice(f32[16,128]{1,0:T(8,128)} %get-tuple-element.777, f32[1,128]{1,0:T(1,128)S(1)} %maximum_add_fusion.5, s32[]{:T(128)} %get-tuple-element.775, s32[]{:T(128)} %constant.104.clone.1..sunk) | dynamic-update-slice | bytes 1028 | tf_op jit(solution)/shard_map/while/body/jit(dynamic_update_index_in_dim)/dynamic_update_slice | solution.py:124
  97.8 1.3 %dynamic_update_slice.5 = f32[16,128]{1,0:T(8,128)} dynamic-update-slice(f32[16,128]{1,0:T(8,128)} %get-tuple-element.777, f32[1,128]{1,0:T(1,128)S(1)} %maximum_add_fusion.5, s32[]{:T(128)} %get-tuple-element.775, s32[]{:T(128)} %constant.104.clone.1..sunk) | dynamic-update-slice | bytes 1028 | tf_op jit(solution)/shard_map/while/body/jit(dynamic_update_index_in_dim)/dynamic_update_slice | solution.py:124
  100.0 1.3 %dynamic_update_slice.5 = f32[16,128]{1,0:T(8,128)} dynamic-update-slice(f32[16,128]{1,0:T(8,128)} %get-tuple-element.777, f32[1,128]{1,0:T(1,128)S(1)} %maximum_add_fusion.5, s32[]{:T(128)} %get-tuple-element.775, s32[]{:T(128)} %constant.104.clone.1..sunk) | dynamic-update-slice | bytes 1028 | tf_op jit(solution)/shard_map/while/body/jit(dynamic_update_index_in_dim)/dynamic_update_slice | solution.py:124
  102.1 1.3 %dynamic_update_slice.5 = f32[16,128]{1,0:T(8,128)} dynamic-update-slice(f32[16,128]{1,0:T(8,128)} %get-tuple-element.777, f32[1,128]{1,0:T(1,128)S(1)} %maximum_add_fusion.5, s32[]{:T(128)} %get-tuple-element.775, s32[]{:T(128)} %constant.104.clone.1..sunk) | dynamic-update-slice | bytes 1028 | tf_op jit(solution)/shard_map/while/body/jit(dynamic_update_index_in_dim)/dynamic_update_slice | solution.py:124
  104.3 1.3 %dynamic_update_slice.5 = f32[16,128]{1,0:T(8,128)} dynamic-update-slice(f32[16,128]{1,0:T(8,128)} %get-tuple-element.777, f32[1,128]{1,0:T(1,128)S(1)} %maximum_add_fusion.5, s32[]{:T(128)} %get-tuple-element.775, s32[]{:T(128)} %constant.104.clone.1..sunk) | dynamic-update-slice | bytes 1028 | tf_op jit(solution)/shard_map/while/body/jit(dynamic_update_index_in_dim)/dynamic_update_slice | solution.py:124
  106.4 1.3 %dynamic_update_slice.5 = f32[16,128]{1,0:T(8,128)} dynamic-update-slice(f32[16,128]{1,0:T(8,128)} %get-tuple-element.777, f32[1,128]{1,0:T(1,128)S(1)} %maximum_add_fusion.5, s32[]{:T(128)} %get-tuple-element.775, s32[]{:T(128)} %constant.104.clone.1..sunk) | dynamic-update-slice | bytes 1028 | tf_op jit(solution)/shard_map/while/body/jit(dynamic_update_index_in_dim)/dynamic_update_slice | solution.py:124
  108.5 1.3 %dynamic_update_slice.5 = f32[16,128]{1,0:T(8,128)} dynamic-update-slice(f32[16,128]{1,0:T(8,128)} %get-tuple-element.777, f32[1,128]{1,0:T(1,128)S(1)} %maximum_add_fusion.5, s32[]{:T(128)} %get-tuple-element.775, s32[]{:T(128)} %constant.104.clone.1..sunk) | dynamic-update-slice | bytes 1028 | tf_op jit(solution)/shard_map/while/body/jit(dynamic_update_index_in_dim)/dynamic_update_slice | solution.py:124
  110.7 1.3 %dynamic_update_slice.5 = f32[16,128]{1,0:T(8,128)} dynamic-update-slice(f32[16,128]{1,0:T(8,128)} %get-tuple-element.777, f32[1,128]{1,0:T(1,128)S(1)} %maximum_add_fusion.5, s32[]{:T(128)} %get-tuple-element.775, s32[]{:T(128)} %constant.104.clone.1..sunk) | dynamic-update-slice | bytes 1028 | tf_op jit(solution)/shard_map/while/body/jit(dynamic_update_index_in_dim)/dynamic_update_slice | solution.py:124
  112.8 1.3 %dynamic_update_slice.5 = f32[16,128]{1,0:T(8,128)} dynamic-update-slice(f32[16,128]{1,0:T(8,128)} %get-tuple-element.777, f32[1,128]{1,0:T(1,128)S(1)} %maximum_add_fusion.5, s32[]{:T(128)} %get-tuple-element.775, s32[]{:T(128)} %constant.104.clone.1..sunk) | dynamic-update-slice | bytes 1028 | tf_op jit(solution)/shard_map/while/body/jit(dynamic_update_index_in_dim)/dynamic_update_slice | solution.py:124
  114.9 1.3 %dynamic_update_slice.5 = f32[16,128]{1,0:T(8,128)} dynamic-update-slice(f32[16,128]{1,0:T(8,128)} %get-tuple-element.777, f32[1,128]{1,0:T(1,128)S(1)} %maximum_add_fusion.5, s32[]{:T(128)} %get-tuple-element.775, s32[]{:T(128)} %constant.104.clone.1..sunk) | dynamic-update-slice | bytes 1028 | tf_op jit(solution)/shard_map/while/body/jit(dynamic_update_index_in_dim)/dynamic_update_slice | solution.py:124
  117.1 1.3 %dynamic_update_slice.5 = f32[16,128]{1,0:T(8,128)} dynamic-update-slice(f32[16,128]{1,0:T(8,128)} %get-tuple-element.777, f32[1,128]{1,0:T(1,128)S(1)} %maximum_add_fusion.5, s32[]{:T(128)} %get-tuple-element.775, s32[]{:T(128)} %constant.104.clone.1..sunk) | dynamic-update-slice | bytes 1028 | tf_op jit(solution)/shard_map/while/body/jit(dynamic_update_index_in_dim)/dynamic_update_slice | solution.py:124
  119.2 1.3 %dynamic_update_slice.5 = f32[16,128]{1,0:T(8,128)} dynamic-update-slice(f32[16,128]{1,0:T(8,128)} %get-tuple-element.777, f32[1,128]{1,0:T(1,128)S(1)} %maximum_add_fusion.5, s32[]{:T(128)} %get-tuple-element.775, s32[]{:T(128)} %constant.104.clone.1..sunk) | dynamic-update-slice | bytes 1028 | tf_op jit(solution)/shard_map/while/body/jit(dynamic_update_index_in_dim)/dynamic_update_slice | solution.py:124
  (381 shorter events, 41.6 us)
Async XLA Ops:
  0.7 3.2 %collective-permute-start = (f32[128]{0:T(128)S(1)}, f32[128]{0:T(128)S(1)}, u32[]{:S(2)}, u32[]{:S(2)}) collective-permute-start(f32[128]{0:T(128)S(1)} %slice_bitcast_fusion), channel_id=1, source_target_pairs={{0,1},{1,2},{2,3},{3,4},{4,5},{5,6},{6,7},{7,8},{8,9},{9,10},{10,1... | collective-permute-start | bytes 1544 | tf_op jit(solution)/shard_map/ppermute | solution.py:13
  3.1 0.6 copy-start.1
  3.7 0.8 copy-start
  3.7 0.8 copy-start.7
  3.7 0.7 copy-start.10
  4.4 0.7 copy-start.9
  5.1 0.7 copy-start.8
  6.2 0.8 copy-start.5
  31.4 13.5 %copy-start.6 = (f32[128,128]{1,0:T(8,128)S(1)}, f32[128,128]{1,0:T(8,128)}, u32[]{:S(2)}) copy-start(f32[128,128]{1,0:T(8,128)} %copy-done.1) | copy-start | bytes 196612
  46.3 17.6 %copy-start.3 = (f32[128,128]{1,0:T(8,128)}, f32[128,128]{1,0:T(8,128)S(1)}, u32[]{:S(2)}) copy-start(f32[128,128]{1,0:T(8,128)S(1)} %get-tuple-element.323) | copy-start | bytes 196612
  69.8 14.5 %copy-start.2 = (f32[128,128]{1,0:T(8,128)S(1)}, f32[128,128]{1,0:T(8,128)}, u32[]{:S(2)}) copy-start(f32[128,128]{1,0:T(8,128)} %copy-done.1) | copy-start | bytes 196612
  84.3 1.4 %copy-start.4 = (f32[128,128]{1,0:T(8,128)S(1)}, f32[128,128]{1,0:T(8,128)}, u32[]{:S(2)}) copy-start(f32[128,128]{1,0:T(8,128)} %copy-done.3) | copy-start | bytes 196612
